TPU v7x, 32 devices: a whole 2x2x4 slice. The times are simulated.
32 devices in a mesh: genome: 8 (over z, x), anc: 4 (over y, core), trait: 1.
Axes of the slice: x: 2, y: 2, z: 4, core: 2. Of those that a mesh axis runs over, the one named last changes fastest.
Arguments:
- coefficients: float32 [4, 128, 16384], P('anc', 'trait', 'genome'), may hold values from -3 to 3
- sumstats: float32 [4, 128, 16384], P('anc', 'trait', 'genome'), may hold values from -12 to 12
- linkage: bfloat16 [4, 16384, 4096], P('anc', 'genome'), may hold values from -0.09375 to 0.09375
- band_start: int32 [4, 64], P('anc', 'genome'), may hold values from 0 to 12288, as said below
- group_ids: int32 [4, 16384], P('anc', 'genome'), may hold values from 0 to 15, never falling along the last dimension, each value on 1 to 8192 neighbouring positions
- group_weight: float32 [4, 16], P('anc'), may hold values from 0.1 to 1.5
- dosage: bfloat16 [4, 2048, 16384], P('anc', None, 'genome'), may hold values from 0 to 2
Outputs:
- updated: float32 [4, 128, 16384], P('anc', 'trait', 'genome')
- scores: float32 [4, 128, 2048], P('anc', 'trait', 'genome')
Inputs may be any that keep to these rules, and one draw needn't show every extreme that they name: band_start[a, u] is the first of the 4096 consecutive SNP columns stored in linkage[a] for row block u, the SNPs u * 256 to u * 256 + 255; these columns always include the block's own SNPs. `group_ids`: group ids never fall along the SNPs of an ancestry, so each group is one run of consecutive SNPs.
All inputs are finite; a program needn't handle non-finite values.
Results may differ from a plain program's by a relative error of at most 0.003.
Values may be sent and summed in bfloat16 or wider, within the bound.
A program may use at most 128 MiB of HBM per device.

v0:
```python
import math

import jax
import jax.numpy as jnp
from jax import lax
from jax.sharding import PartitionSpec as P

TRAITS = 128
TILE = 256


step_size = 0.5
merging = 0.5
epsilon = 1e-06


def passed_along(block, axis, distance):
    devices = range(lax.axis_size(axis))
    route = [(i - distance, i) for i in devices if i - distance in devices]
    return lax.ppermute(block, axis, route)


def per_device(coefficients, sumstats, linkage, band_start, group_ids, group_weight, dosage):
    current = coefficients[0]
    targets = sumstats[0]
    band = linkage[0]
    starts = band_start[0]
    group_list = group_ids[0]
    weights = group_weight[0]
    genotype = dosage[0]
    traits_here, snp_rows = current.shape
    band_width = band.shape[1]
    reach_count = band_width // snp_rows
    genome_count = lax.axis_size("genome")
    position = lax.axis_index("genome")
    anchor = position * snp_rows
    ancestries = lax.axis_size("anc") * coefficients.shape[0]
    mean_coef = lax.psum(current, "anc") / ancestries
    low_copy = current.astype(jnp.bfloat16)
    below_list = []
    above_list = []
    for distance in range(1, reach_count + 1):
        below_list.insert(0, passed_along(low_copy, "genome", distance))
        above_list.append(passed_along(low_copy, "genome", -distance))
    extended = jnp.concatenate(below_list + [low_copy] + above_list, axis=1)
    local_start = starts - anchor + band_width
    windows = jax.vmap(
        lambda begin_at: lax.dynamic_slice_in_dim(extended, begin_at, band_width, 1)
    )(local_start)
    band_tiles = band.reshape(snp_rows // TILE, TILE, band_width)
    products = jnp.einsum("ntw,nrw->tnr", windows, band_tiles, preferred_element_type=jnp.float32)
    band_product = products.reshape(traits_here, snp_rows)
    gradient = current + band_product - targets + merging * (current - mean_coef)
    proposal = current - step_size * gradient
    trait_part = jnp.sum(proposal * proposal, axis=0)
    trait_total = lax.psum(trait_part, "trait")
    same_group = (group_list[:, None] == group_list[None, :]).astype(jnp.float32)
    local_squares = jnp.dot(same_group, trait_total, precision=lax.Precision.HIGHEST)
    local_counts = jnp.sum(same_group, axis=1)
    id_float = group_list.astype(jnp.float32)
    first_id = id_float[0]
    last_id = id_float[-1]
    edge_values = (
        lax.all_gather(first_id[None], "genome", axis=0, tiled=True),
        lax.all_gather(last_id[None], "genome", axis=0, tiled=True),
        lax.all_gather(local_squares[:1], "genome", axis=0, tiled=True),
        lax.all_gather(local_counts[:1], "genome", axis=0, tiled=True),
        lax.all_gather(local_squares[-1:], "genome", axis=0, tiled=True),
        lax.all_gather(local_counts[-1:], "genome", axis=0, tiled=True),
    )
    firsts, lasts, head_squares, head_counts, tail_squares, tail_counts = edge_values
    others = (jnp.arange(genome_count, dtype=jnp.int32) != position)[None, :]
    at_head = id_float[:, None] == firsts[None, :]
    at_tail = id_float[:, None] == lasts[None, :]
    square_terms = jnp.where(
        at_head, head_squares[None, :], jnp.where(at_tail, tail_squares[None, :], 0.0)
    )
    count_terms = jnp.where(
        at_head, head_counts[None, :], jnp.where(at_tail, tail_counts[None, :], 0.0)
    )
    extra_squares = jnp.sum(jnp.where(others, square_terms, 0.0), axis=1)
    extra_counts = jnp.sum(jnp.where(others, count_terms, 0.0), axis=1)
    group_squares = local_squares + extra_squares
    group_counts = local_counts + extra_counts
    lookup = (group_list[:, None] == jnp.arange(weights.shape[0], dtype=jnp.int32)[None, :]).astype(
        jnp.float32
    )
    snp_weight = jnp.dot(lookup, weights, precision=lax.Precision.HIGHEST)
    threshold = step_size * snp_weight * jnp.sqrt(group_counts * TRAITS)
    factor = jnp.maximum(0.0, 1.0 - threshold / jnp.sqrt(group_squares + epsilon))
    updated = proposal * factor[None, :]
    snps_total = snp_rows * genome_count
    partial_value = lax.dot_general(
        updated.astype(jnp.bfloat16),
        genotype,
        (((1,), (1,)), ((), ())),
        preferred_element_type=jnp.float32,
    ) / math.sqrt(snps_total)
    scores = lax.psum_scatter(partial_value, "genome", scatter_dimension=1, tiled=True)
    return (updated[None], scores[None])


def solution(mesh):
    in_specs = (
        P("anc", "trait", "genome"),
        P("anc", "trait", "genome"),
        P("anc", "genome", None),
        P("anc", "genome"),
        P("anc", "genome"),
        P("anc", None),
        P("anc", None, "genome"),
    )
    out_specs = (P("anc", "trait", "genome"), P("anc", "trait", "genome"))
    return jax.shard_map(
        per_device, mesh=mesh, in_specs=in_specs, out_specs=out_specs, check_vma=False
    )
```

profile of v0, /device:TPU:0, one launch (start us, length us, event | category | flops | bytes accessed | tf_op | source)
XLA Modules:
  0.0 200.8 jit_solution(4251630747943932448)
XLA Ops:
  7.2 1.5 copy.14
  8.9 5.8 %collective-permute-start = (bf16[128,2048]{0,1:T(8,128)(2,1)S(1)}, bf16[128,2048]{0,1:T(8,128)(2,1)}, u32[]{:S(2)}, u32[]{:S(2)}) collective-permute-start(bf16[128,2048]{0,1:T(8,128)(2,1)S(1)} %bitcast_convert_fusion), channel_id=1, source_target_pairs={{0,8},{4,12},{8,16},{12,20},{16,24},{20,28},{1,9},{5,13},{9,17},{1... | collective-permute-start | bytes 1572872 | tf_op jit(solution)/shard_map/ppermute | solution.py:20
  14.7 4.3 %collective-permute-start.1 = (bf16[128,2048]{0,1:T(8,128)(2,1)S(1)}, bf16[128,2048]{0,1:T(8,128)(2,1)}, u32[]{:S(2)}, u32[]{:S(2)}) collective-permute-start(bf16[128,2048]{0,1:T(8,128)(2,1)S(1)} %bitcast_convert_fusion), channel_id=1, source_target_pairs={{0,4},{4,8},{8,12},{12,16},{16,20},{20,24},{24,28},{1,5},{5,9},{9,... | collective-permute-start | bytes 1572872 | tf_op jit(solution)/shard_map/ppermute | solution.py:20
  18.9 1.3 collective-permute-start.2
  20.2 1.3 collective-permute-start.3
  21.6 2.5 %fusion.2 = f32[2048]{0:T(1024)S(1)} fusion(s32[2048]{0:T(1024)} %bitcast.57), kind=kLoop, calls=%fused_computation.6 | loop fusion | flops 12580864 | bytes 16384 | tf_op jit(solution)/shard_map/reduce_sum | solution.py:59
  24.9 1.5 copy.17
  27.1 1.3 dynamic-slice.4
  31.8 1.4 fusion.13
  34.3 5.9 %collective-permute-done.1 = bf16[128,2048]{0,1:T(8,128)(2,1)} collective-permute-done((bf16[128,2048]{0,1:T(8,128)(2,1)S(1)}, bf16[128,2048]{0,1:T(8,128)(2,1)}, u32[]{:S(2)}, u32[]{:S(2)}) %collective-permute-start.1) | collective-permute-done | bytes 524320 | tf_op jit(solution)/shard_map/ppermute | solution.py:20
  40.2 1.1 constant_dynamic-update-slice_fusion.3
  41.3 1.3 constant_dynamic-update-slice_fusion.2
  42.6 1.1 constant_dynamic-update-slice_fusion.1
  44.6 1.6 copy-done.3
  46.1 35.2 %while.1 = (s32[]{:T(128)}, bf16[128,10240]{0,1:T(8,128)(2,1)}, s32[8,2]{0,1:T(2,128)S(1)}, bf16[8,128,4096]{2,1,0:T(8,128)(2,1)}, s32[]{:T(128)}) while((s32[]{:T(128)}, bf16[128,10240]{0,1:T(8,128)(2,1)}, s32[8,2]{0,1:T(2,128)S(1)}, bf16[8,128,4096]{2,1,0:T(8,128)(2,1)}, s32[]{:T(128)}) %tuple.33), condition=%wide.while_cond, body=%wide.while_body.sunk | while | flops 2 | bytes 6292061 | solution.py:48
  46.8 2.2 %constant_dynamic-slice_fusion.5 = bf16[128,4096]{0,1:T(8,128)(2,1)S(1)} fusion(bf16[128,10240]{0,1:T(8,128)(2,1)} %get-tuple-element.76, s32[]{:T(128)} %bitcast.53), kind=kLoop, calls=%fused_computation.2.clone.1 | loop fusion | bytes 2097156 | tf_op jit(solution)/shard_map/vmap()/gather
  51.2 2.1 %constant_dynamic-slice_fusion.5 = bf16[128,4096]{0,1:T(8,128)(2,1)S(1)} fusion(bf16[128,10240]{0,1:T(8,128)(2,1)} %get-tuple-element.76, s32[]{:T(128)} %bitcast.53), kind=kLoop, calls=%fused_computation.2.clone.1 | loop fusion | bytes 2097156 | tf_op jit(solution)/shard_map/vmap()/gather
  53.9 1.1 bitcast_dynamic-update-slice_fusion.2
  55.7 2.1 %constant_dynamic-slice_fusion.5 = bf16[128,4096]{0,1:T(8,128)(2,1)S(1)} fusion(bf16[128,10240]{0,1:T(8,128)(2,1)} %get-tuple-element.76, s32[]{:T(128)} %bitcast.53), kind=kLoop, calls=%fused_computation.2.clone.1 | loop fusion | bytes 2097156 | tf_op jit(solution)/shard_map/vmap()/gather
  60.1 2.1 %constant_dynamic-slice_fusion.5 = bf16[128,4096]{0,1:T(8,128)(2,1)S(1)} fusion(bf16[128,10240]{0,1:T(8,128)(2,1)} %get-tuple-element.76, s32[]{:T(128)} %bitcast.53), kind=kLoop, calls=%fused_computation.2.clone.1 | loop fusion | bytes 2097156 | tf_op jit(solution)/shard_map/vmap()/gather
  64.4 2.1 %constant_dynamic-slice_fusion.5 = bf16[128,4096]{0,1:T(8,128)(2,1)S(1)} fusion(bf16[128,10240]{0,1:T(8,128)(2,1)} %get-tuple-element.76, s32[]{:T(128)} %bitcast.53), kind=kLoop, calls=%fused_computation.2.clone.1 | loop fusion | bytes 2097156 | tf_op jit(solution)/shard_map/vmap()/gather
  68.8 2.1 %constant_dynamic-slice_fusion.5 = bf16[128,4096]{0,1:T(8,128)(2,1)S(1)} fusion(bf16[128,10240]{0,1:T(8,128)(2,1)} %get-tuple-element.76, s32[]{:T(128)} %bitcast.53), kind=kLoop, calls=%fused_computation.2.clone.1 | loop fusion | bytes 2097156 | tf_op jit(solution)/shard_map/vmap()/gather
  73.2 2.1 %constant_dynamic-slice_fusion.5 = bf16[128,4096]{0,1:T(8,128)(2,1)S(1)} fusion(bf16[128,10240]{0,1:T(8,128)(2,1)} %get-tuple-element.76, s32[]{:T(128)} %bitcast.53), kind=kLoop, calls=%fused_computation.2.clone.1 | loop fusion | bytes 2097156 | tf_op jit(solution)/shard_map/vmap()/gather
  77.7 2.1 %constant_dynamic-slice_fusion.5 = bf16[128,4096]{0,1:T(8,128)(2,1)S(1)} fusion(bf16[128,10240]{0,1:T(8,128)(2,1)} %get-tuple-element.76, s32[]{:T(128)} %bitcast.53), kind=kLoop, calls=%fused_computation.2.clone.1 | loop fusion | bytes 2097156 | tf_op jit(solution)/shard_map/vmap()/gather
  81.4 11.3 %convolution_bitcast_fusion = f32[128,8,256]{2,0,1:T(8,128)S(1)} fusion(bf16[8,128,4096]{2,1,0:T(8,128)(2,1)} %get-tuple-element.9, bf16[8,256,4096]{2,1,0:T(8,128)(2,1)} %bitcast.55), kind=kOutput, calls=%fused_computation.12 | convolution fusion | flops 2147483648 | bytes 26214400 | tf_op jit(solution)/shard_map/ntw,nrw->tnr/dot_general | solution.py:51
  92.6 1.3 copy.16
  94.0 2.1 %multiply_reduce_fusion = (f32[2048]{0:T(1024)S(1)}, f32[128,2048]{0,1:T(8,128)S(1)}) fusion(f32[128,2048]{0,1:T(8,128)} %all-reduce.10.cloned.1.call-done, f32[1,128,2048]{1,2,0:T(8,128)S(1)} %copy.17, f32[128,8,256]{0,2,1:T(8,128)} %copy.16, f32[1,128,2048]{1,2,0:T(8,128)S(1)} %copy-done.2), kind=kLoop, calls=%fused_computation.18 | loop fusion | flops 2619392 | bytes 5251072 | tf_op jit(solution)/shard_map/reduce_sum | solution.py:55
  96.1 6.9 %fusion = f32[1,2048]{1,0:T(1,128)S(1)} fusion(f32[2048,1]{0,1:T(1,128)S(1)} %bitcast.56, s32[2048]{0:T(1024)S(1)} %bitcast.60), kind=kOutput, calls=%fused_computation.3 | convolution fusion | flops 54525952 | bytes 24576 | tf_op jit(solution)/shard_map/dot_general | solution.py:58
  104.7 19.2 %all-reduce.7 = (f32[8]{0:T(128)S(1)}, f32[8]{0:T(128)S(1)}, f32[8]{0:T(128)S(1)}, f32[8]{0:T(128)S(1)}, f32[8]{0:T(128)S(1)}, /*index=5*/f32[8]{0:T(128)S(1)}) all-reduce(f32[8]{0:T(128)S(1)} %slice_dynamic-update-slice_fusion.2, f32[8]{0:T(128)S(1)} %slice_dynamic-update-slice_fusion.4, ...), channel_id=1, replica_groups=mesh['genome'=8,'anc'=4,'trait'=1] {'genome'}, use_global_device_ids=true, to_apply=%add.4 | all-reduce | flops 48 | bytes 384
  124.0 7.7 %fusion.7 = f32[128,2048]{1,0:T(8,128)} fusion(bf16[1,2048,2048]{2,1,0:T(8,128)(2,1)} %param.13, f32[128,2048]{0,1:T(8,128)S(1)} %get-tuple-element.39, f32[2048]{0:T(1024)S(1)} %subtract_maximum_fusion), kind=kOutput, calls=%fused_computation.11 | convolution fusion | flops 1074528256 | bytes 10493952 | tf_op jit(solution)/shard_map/dot_general | solution.py:93
  132.1 1.3 copy.18
  133.4 60.5 %reduce-scatter.2.cloned.1.call-done = f32[128,256]{1,0:T(8,128)} async-done(((f32[128,2048]{1,0:T(8,128)}), f32[128,256]{1,0:T(8,128)}) %reduce-scatter.2.cloned.1.call-update) | async-done | bytes 131088 | tf_op jit(solution)/shard_map/reduce_scatter | solution.py:99
  (71 shorter events, 25.8 us)
Async XLA Ops:
  7.2 24.6 %copy-start = (f32[1,16]{1,0:T(1,128)S(1)}, f32[1,16]{1,0:T(1,128)}, u32[]{:S(2)}) copy-start(f32[1,16]{1,0:T(1,128)} %param.12) | copy-start | bytes 196
  7.2 86.8 %all-reduce.10.cloned.1.call-start = ((), (), s32[]{:S(2)}) async-start(), calls=%async_computation.1 | async-start | bytes 2097152 | tf_op jit(solution)/shard_map/psum | solution.py:38
  8.8 12.7 %copy-start.1 = (f32[1,128,2048]{1,2,0:T(8,128)}, f32[1,128,2048]{1,2,0:T(8,128)S(1)}, u32[]{:S(2)}) copy-start(f32[1,128,2048]{1,2,0:T(8,128)S(1)} %copy.14) | copy-start | bytes 3145732
  8.9 24.3 %collective-permute-start = (bf16[128,2048]{0,1:T(8,128)(2,1)S(1)}, bf16[128,2048]{0,1:T(8,128)(2,1)}, u32[]{:S(2)}, u32[]{:S(2)}) collective-permute-start(bf16[128,2048]{0,1:T(8,128)(2,1)S(1)} %bitcast_convert_fusion), channel_id=1, source_target_pairs={{0,8},{4,12},{8,16},{12,20},{16,24},{20,28},{1,9},{5,13},{9,17},{1... | collective-permute-start | bytes 1572872 | tf_op jit(solution)/shard_map/ppermute | solution.py:20
  14.7 25.5 %collective-permute-start.1 = (bf16[128,2048]{0,1:T(8,128)(2,1)S(1)}, bf16[128,2048]{0,1:T(8,128)(2,1)}, u32[]{:S(2)}, u32[]{:S(2)}) collective-permute-start(bf16[128,2048]{0,1:T(8,128)(2,1)S(1)} %bitcast_convert_fusion), channel_id=1, source_target_pairs={{0,4},{4,8},{8,12},{12,16},{16,20},{20,24},{24,28},{1,5},{5,9},{9,... | collective-permute-start | bytes 1572872 | tf_op jit(solution)/shard_map/ppermute | solution.py:20
  18.9 23.7 %collective-permute-start.2 = (bf16[128,2048]{0,1:T(8,128)(2,1)S(1)}, bf16[128,2048]{0,1:T(8,128)(2,1)}, u32[]{:S(2)}, u32[]{:S(2)}) collective-permute-start(bf16[128,2048]{0,1:T(8,128)(2,1)S(1)} %bitcast_convert_fusion), channel_id=1, source_target_pairs={{4,0},{8,4},{12,8},{16,12},{20,16},{24,20},{28,24},{5,1},{9,5},{13... | collective-permute-start | bytes 1572872 | tf_op jit(solution)/shard_map/ppermute | solution.py:20
  20.2 24.3 %collective-permute-start.3 = (bf16[128,2048]{0,1:T(8,128)(2,1)S(1)}, bf16[128,2048]{0,1:T(8,128)(2,1)S(1)}, u32[]{:S(2)}, u32[]{:S(2)}) collective-permute-start(bf16[128,2048]{0,1:T(8,128)(2,1)S(1)} %bitcast_convert_fusion), channel_id=1, source_target_pairs={{8,0},{12,4},{16,8},{20,12},{24,16},{28,20},{9,1},{13,5},{17,9},{2... | collective-permute-start | bytes 1572872 | tf_op jit(solution)/shard_map/ppermute | solution.py:20
  21.6 172.4 %reduce-scatter.2.cloned.1.call-start = ((), (), s32[]{:S(2)}) async-start(), calls=%async_computation.2 | async-start | bytes 1179648 | tf_op jit(solution)/shard_map/reduce_scatter | solution.py:99
  44.6 1.6 copy-start.3
  81.4 12.6 %copy-start.2 = (f32[1,128,2048]{1,2,0:T(8,128)S(1)}, f32[1,128,2048]{1,2,0:T(8,128)}, u32[]{:S(2)}) copy-start(f32[1,128,2048]{1,2,0:T(8,128)} %copy-done.1) | copy-start | bytes 3145732
  81.4 14.7 %copy-start.4 = (s32[1,2048]{1,0:T(1,128)S(1)}, s32[1,2048]{1,0:T(1,128)}, u32[]{:S(2)}) copy-start(s32[1,2048]{1,0:T(1,128)} %param.11) | copy-start | bytes 24580
Sparse Core Ops, SparseCore 0:
  21.7 38.0 all-reduce.9
  131.9 61.9 reduce-scatter.1
where the time goes:
time: 202 us; the launch traced here: 201 us
  waiting for transfers between devices  67.2 us (33%)
  local copies, waits for them, and re-layouts  52.1 us (26%)
  matrix products  27.3 us (14%)
  blocking collectives  19.2 us (10%)
  between operations  14.2 us (7%)
  starting transfers between devices  12.7 us (6%)
  other arithmetic  7.88 us (4%)
    reduce_scatter x1, waiting for transfers between devices, per_device(): lax.psum_scatter(partial_value, 'genome', scatter_dimension=1, tiled=True)  60.5 us
    gather x40, local copies, waits for them, and re-layouts  35.1 us
    unnamed x1, blocking collectives  19.2 us
    unnamed x29, local copies, waits for them, and re-layouts  15.6 us
    ppermute x4, starting transfers between devices, passed_along(): return lax.ppermute(block, axis, route)  12.6 us
    dot_general x1, matrix products, per_device(): jnp.einsum('ntw,nrw->tnr', windows, band_tiles, preferred_element_type=jn...  11.3 us
    dot_general x1, matrix products, per_device(): lax.dot_general(updated.astype(jnp.bfloat16), genotype, (((1,), (1,)), ((...  7.74 us
    dot_general x1, matrix products, per_device(): jnp.dot(same_group, trait_total, precision=lax.Precision.HIGHEST)  6.93 us
  transfers between devices with their start and end apart: 6, of which 3 were waited for; matrix products, arithmetic and copies ran while one was open for 33% of the time, Pallas kernels for 0%

commit v1 on v0

v1 whole, which is shorter than its diff:
```python
import functools
import math

import jax
import jax.numpy as jnp
from jax import lax
from jax.experimental import pallas as pl
from jax.experimental.pallas import tpu as pltpu
from jax.sharding import PartitionSpec as P

step_size = 0.5
merging = 0.5
epsilon = 1e-06

MESH = pl.DeviceIdType.MESH
F32 = jnp.float32
BF16 = jnp.bfloat16


def step_kernel(
    sizes,
    coef_hbm, sums_hbm, link_hbm, starts_ref, ids_ref, weight_ref, dosage_hbm,
    updated_hbm, score_ref,
    coef, sums, link, dosage, low, ext, extf, peers, proposal, updated, updated_t, row,
    stats_out, stats_in, part_out, part_in,
    load_sem, link_sem, store_sem,
    halo_send, halo_recv, anc_send, anc_recv, stats_send, stats_recv, part_send, part_recv,
):
    genomes, ancs, traits_n, reach, tile, groups = sizes
    traits_here, snps = coef.shape
    width = link.shape[1]
    tiles = snps // tile
    persons_per = part_out.shape[1]
    g = lax.axis_index("genome")
    a = lax.axis_index("anc")
    t = lax.axis_index("trait")
    stat_peers = [(k, m) for m in range(traits_n) for k in range(genomes) if (k, m) != (0, 0)]

    def genome_peer(k):
        return lax.rem(g + k, genomes)

    load_coef = pltpu.make_async_copy(coef_hbm.at[0], coef, load_sem.at[0])
    load_coef.start()
    barrier = pltpu.get_barrier_semaphore()
    for k, m in stat_peers:
        pl.semaphore_signal(
            barrier, inc=1, device_id_type=MESH,
            device_id={"genome": genome_peer(k), "trait": lax.rem(t + m, traits_n)},
        )
    for k in range(1, ancs):
        pl.semaphore_signal(
            barrier, inc=1, device_id={"anc": lax.rem(a + k, ancs)}, device_id_type=MESH
        )
    load_sums = pltpu.make_async_copy(sums_hbm.at[0], sums, load_sem.at[1])
    load_sums.start()
    load_dosage = pltpu.make_async_copy(dosage_hbm.at[0], dosage, load_sem.at[2])

    def link_copy(u):
        rows = pl.ds(pl.multiple_of(u * tile, tile), tile)
        return pltpu.make_async_copy(link_hbm.at[0, rows, :], link.at[rows, :], link_sem.at[u])

    load_coef.wait()

    def own_block(u, carry):
        cols = pl.ds(pl.multiple_of(u * tile, tile), tile)
        block = coef[:, cols].astype(BF16)
        low[:, cols] = block
        flat = block.astype(F32).T
        extf[pl.ds(pl.multiple_of(reach * snps + u * tile, tile), tile), :] = flat
        ext[reach, cols, :] = flat.astype(BF16)
        return carry

    lax.fori_loop(0, tiles, own_block, 0)
    pl.semaphore_wait(barrier, len(stat_peers) + ancs - 1)

    distances = [d for far in range(1, reach + 1) for d in (far, -far)]

    def halo_copy(d):
        slot = reach - d
        return pltpu.make_async_remote_copy(
            src_ref=ext.at[reach], dst_ref=ext.at[slot],
            send_sem=halo_send.at[slot], recv_sem=halo_recv.at[slot],
            device_id={"genome": jnp.clip(g + d, 0, genomes - 1)}, device_id_type=MESH,
        )

    def in_range(p):
        return jnp.logical_and(p >= 0, p < genomes)

    for d in distances:
        @pl.when(in_range(g + d))
        def _(d=d):
            halo_copy(d).start()

    def anc_copy(k):
        return pltpu.make_async_remote_copy(
            src_ref=low, dst_ref=peers.at[k - 1],
            send_sem=anc_send.at[k - 1], recv_sem=anc_recv.at[k - 1],
            device_id={"anc": lax.rem(a + k, ancs)}, device_id_type=MESH,
        )

    for k in range(1, ancs):
        anc_copy(k).start()
    for u in range(tiles):
        link_copy(u).start()
    load_dosage.start()
    load_sums.wait()

    for d in distances:
        slot = reach - d
        chunk = 256

        @pl.when(in_range(g - d))
        def _(d=d, slot=slot):
            halo_copy(d).wait_recv()

            def widen(i, carry):
                at = pl.multiple_of(i * chunk, chunk)
                extf[pl.ds(pl.multiple_of(slot * snps + at, chunk), chunk), :] = (
                    ext[slot, pl.ds(at, chunk), :].astype(F32)
                )
                return carry

            lax.fori_loop(0, snps // chunk, widen, 0)

        @pl.when(jnp.logical_not(in_range(g - d)))
        def _(slot=slot):
            def clear(i, carry):
                at = pl.multiple_of(slot * snps + i * chunk, chunk)
                extf[pl.ds(at, chunk), :] = jnp.zeros((chunk, traits_here), F32)
                return carry

            lax.fori_loop(0, snps // chunk, clear, 0)

    for k in range(1, ancs):
        anc_copy(k).wait_recv()

    def band_tile(u, carry):
        link_copy(u).wait()
        rows = pl.ds(pl.multiple_of(u * tile, tile), tile)
        begin = jnp.clip(starts_ref[0, u] - g * snps + reach * snps, 0, extf.shape[0] - width)
        depth = 512
        total = jnp.zeros((tile, traits_here), F32)
        for c in range(0, width, depth):
            window = extf[pl.ds(begin + c, depth), :].astype(BF16)
            total = total + jnp.dot(
                link[rows, c:c + depth], window, preferred_element_type=F32
            )
        band = total.T
        current = coef[:, rows]
        mean = current
        for k in range(1, ancs):
            mean = mean + peers[k - 1, :, rows].astype(F32)
        mean = mean / ancs
        gradient = current + band - sums[:, rows] + merging * (current - mean)
        value = current - step_size * gradient
        proposal[:, rows] = value
        row[:, rows] = jnp.sum(value * value, axis=0, keepdims=True)
        return carry

    lax.fori_loop(0, tiles, band_tile, 0)

    group_of = lax.broadcasted_iota(jnp.int32, (groups, snps), 0)
    mine = group_of == ids_ref[...]
    squares = jnp.sum(jnp.where(mine, row[...], 0.0), axis=1, keepdims=True)
    counts = jnp.sum(jnp.where(mine, 1.0, 0.0), axis=1, keepdims=True)
    lane = lax.broadcasted_iota(jnp.int32, (groups, 128), 1)
    stats = jnp.where(lane == 0, squares, jnp.where(lane == 1, counts, 0.0))
    stats_out[...] = stats

    def stats_copy(i):
        k, m = stat_peers[i]
        return pltpu.make_async_remote_copy(
            src_ref=stats_out, dst_ref=stats_in.at[i],
            send_sem=stats_send.at[i], recv_sem=stats_recv.at[i],
            device_id={"genome": genome_peer(k), "trait": lax.rem(t + m, traits_n)},
            device_id_type=MESH,
        )

    for i in range(len(stat_peers)):
        stats_copy(i).start()
    load_dosage.wait()
    for i in range(len(stat_peers)):
        stats_copy(i).wait_recv()
        stats = stats + stats_in[i]
    all_squares = stats[:, 0:1]
    all_counts = stats[:, 1:2] / traits_n
    square_of = lax.broadcasted_iota(jnp.int32, (groups, groups), 0)
    lane_of = lax.broadcasted_iota(jnp.int32, (groups, groups), 1)
    weight = jnp.sum(
        jnp.where(square_of == lane_of, weight_ref[...], 0.0), axis=1, keepdims=True
    )
    threshold = step_size * weight * jnp.sqrt(all_counts * (traits_here * traits_n))
    shrink = jnp.maximum(0.0, 1.0 - threshold / jnp.sqrt(all_squares + epsilon))
    row[...] = jnp.sum(jnp.where(mine, shrink, 0.0), axis=0, keepdims=True)

    def shrink_tile(u, carry):
        cols = pl.ds(pl.multiple_of(u * tile, tile), tile)
        value = proposal[:, cols] * row[:, cols]
        updated[:, cols] = value
        updated_t[cols, :] = value.T.astype(BF16)
        return carry

    lax.fori_loop(0, tiles, shrink_tile, 0)
    store = pltpu.make_async_copy(updated, updated_hbm.at[0], store_sem)
    store.start()

    scale = 1.0 / math.sqrt(snps * genomes)

    def partial(k):
        at = pl.ds(pl.multiple_of(genome_peer(k) * persons_per, persons_per), persons_per)
        return jnp.dot(dosage[at, :], updated_t[...], preferred_element_type=F32) * scale

    def part_copy(k):
        return pltpu.make_async_remote_copy(
            src_ref=part_out.at[k - 1], dst_ref=part_in.at[k - 1],
            send_sem=part_send.at[k - 1], recv_sem=part_recv.at[k - 1],
            device_id={"genome": genome_peer(k)}, device_id_type=MESH,
        )

    def send_part(k, carry):
        part_out[k - 1] = partial(k).astype(BF16)
        part_copy(k).start()
        return carry

    lax.fori_loop(1, genomes, send_part, 0)

    def add_part(k, total):
        part_copy(k).wait_recv()
        return total + part_in[k - 1].astype(F32)

    score_ref[0] = lax.fori_loop(1, genomes, add_part, partial(0)).T

    store.wait()
    for d in distances:
        @pl.when(in_range(g + d))
        def _(d=d):
            halo_copy(d).wait_send()
    for k in range(1, ancs):
        anc_copy(k).wait_send()
    for i in range(len(stat_peers)):
        stats_copy(i).wait_send()

    def sent_part(k, carry):
        part_copy(k).wait_send()
        return carry

    lax.fori_loop(1, genomes, sent_part, 0)


def per_device(coefficients, sumstats, linkage, band_start, group_ids, group_weight, dosage):
    _, traits_here, snps = coefficients.shape
    width = linkage.shape[2]
    genomes = lax.axis_size("genome")
    ancs = lax.axis_size("anc")
    traits_n = lax.axis_size("trait")
    persons = dosage.shape[1]
    persons_per = persons // genomes
    groups = group_weight.shape[1]
    reach = -(-width // snps)
    tile = snps // band_start.shape[1]
    slots = 2 * reach + 1
    stat_n = genomes * traits_n - 1
    sizes = (genomes, ancs, traits_n, reach, tile, groups)
    anyspace = pl.BlockSpec(memory_space=pl.ANY)
    vmem = pl.BlockSpec(memory_space=pltpu.VMEM)
    smem = pl.BlockSpec(memory_space=pltpu.SMEM)
    dma = pltpu.SemaphoreType.DMA
    return pl.pallas_call(
        functools.partial(step_kernel, sizes),
        out_shape=(
            jax.ShapeDtypeStruct((1, traits_here, snps), F32),
            jax.ShapeDtypeStruct((1, traits_here, persons_per), F32),
        ),
        in_specs=[anyspace, anyspace, anyspace, smem, vmem, vmem, anyspace],
        out_specs=(anyspace, vmem),
        scratch_shapes=[
            pltpu.VMEM((traits_here, snps), F32),
            pltpu.VMEM((traits_here, snps), F32),
            pltpu.VMEM((snps, width), BF16),
            pltpu.VMEM((persons, snps), BF16),
            pltpu.VMEM((traits_here, snps), BF16),
            pltpu.VMEM((slots, snps, traits_here), BF16),
            pltpu.VMEM((slots * snps, traits_here), F32),
            pltpu.VMEM((ancs - 1, traits_here, snps), BF16),
            pltpu.VMEM((traits_here, snps), F32),
            pltpu.VMEM((traits_here, snps), F32),
            pltpu.VMEM((snps, traits_here), BF16),
            pltpu.VMEM((1, snps), F32),
            pltpu.VMEM((groups, 128), F32),
            pltpu.VMEM((stat_n, groups, 128), F32),
            pltpu.VMEM((genomes - 1, persons_per, traits_here), BF16),
            pltpu.VMEM((genomes - 1, persons_per, traits_here), BF16),
            dma((3,)), dma((snps // tile,)), dma,
            dma((slots,)), dma((slots,)), dma((ancs - 1,)), dma((ancs - 1,)),
            dma((stat_n,)), dma((stat_n,)), dma((genomes - 1,)), dma((genomes - 1,)),
        ],
        compiler_params=pltpu.CompilerParams(
            collective_id=0, has_side_effects=True, vmem_limit_bytes=56 * 1024 * 1024
        ),
    )(coefficients, sumstats, linkage, band_start, group_ids, group_weight, dosage)


def solution(mesh):
    in_specs = (
        P("anc", "trait", "genome"),
        P("anc", "trait", "genome"),
        P("anc", "genome", None),
        P("anc", "genome"),
        P("anc", "genome"),
        P("anc", None),
        P("anc", None, "genome"),
    )
    out_specs = (P("anc", "trait", "genome"), P("anc", "trait", "genome"))
    return jax.shard_map(
        per_device, mesh=mesh, in_specs=in_specs, out_specs=out_specs, check_vma=False
    )
```

time: 202 us -> 60.6 us (0.30)
  waiting for transfers between devices: 67.2 us -> 0 us
  Pallas kernels: 0 us -> 55 us
  local copies, waits for them, and re-layouts: 52.1 us -> 3.86 us
  matrix products: 27.3 us -> 0 us
  blocking collectives: 19.2 us -> 0 us
  between operations: 14.2 us -> 0.64 us
  starting transfers between devices: 12.7 us -> 0 us
  other arithmetic: 7.88 us -> 0 us
    reduce_scatter x1 -> x0, waiting for transfers between devices: 60.5 us -> none  [per_device(): lax.psum_scatter(partial_value, 'genome', scatter_dimension=1, tiled=True)]
    pallas_call x0 -> x1, Pallas kernels: none -> 55 us  [per_device(): pl.pallas_call(functools.partial(step_kernel, sizes), out_shape=(jax.Shap...]
    gather x40 -> x0, local copies, waits for them, and re-layouts: 35.1 us -> none
    dot_general x4 -> x0, matrix products: 27.3 us -> none  [the longest x1 11.3 us: per_device(): jnp.einsum('ntw,nrw->tnr', windows, band_tiles, preferred_element_type=jn...]
    unnamed x1 -> x0, blocking collectives: 19.2 us -> none
    ppermute x4 -> x0, starting transfers between devices: 12.6 us -> none  [passed_along(): return lax.ppermute(block, axis, route)]
    unnamed x29 -> x2, local copies, waits for them, and re-layouts: 15.6 us -> 3.86 us
    ppermute x4 -> x0, waiting for transfers between devices: 6.64 us -> none  [passed_along(): return lax.ppermute(block, axis, route)]
  transfers between devices with their start and end apart: 6 -> 0, of which waited for: 3 -> 0; matrix products, arithmetic and copies ran while one was open for 33% -> 0% of each run, Pallas kernels for 0% -> 0%
where the time goes in v1:
time: 60.6 us; the launch traced here: 59.5 us
  Pallas kernels  55 us (91%)
  local copies, waits for them, and re-layouts  3.86 us (6%)
  between operations  0.64 us (1%)
    pallas_call x1, Pallas kernels, per_device(): pl.pallas_call(functools.partial(step_kernel, sizes), out_shape=(jax.Shap...  55 us
    unnamed x2, local copies, waits for them, and re-layouts  3.86 us

profile of v1, /device:TPU:0, one launch (start us, length us, event | category | flops | bytes accessed | tf_op | source)
XLA Modules:
  0.0 59.5 jit_solution(6303631503018642677)
XLA Ops:
  0.6 55.0 %shard_map.86 = (f32[1,128,2048]{2,1,0:T(8,128)}, f32[1,128,256]{2,1,0:T(8,128)}) custom-call(f32[1,128,2048]{2,1,0:T(8,128)} %coef_hbm.1, f32[1,128,2048]{2,1,0:T(8,128)} %sums_hbm.1, bf16[1,2048,4096]{2,1,0:T(8,128)(2,1)} %link_hbm.1, s32[1,8]{1,0:T(1,128)} %starts_ref.1, s32[1,2048]{1,0:T(1,128)} %ids_ref.1, f32[1,16]{1,0:T(1,128)} %weight_ref.1, ...), custom_call_target="tpu_custom_call" | custom-call | tf_op jit(solution)/shard_map/pallas_call | solution.py:268
  55.7 2.3 %copy.11 = f32[1,128,2048]{2,1,0:T(8,128)} copy(f32[1,128,2048]{2,1,0:T(8,128)} %get-tuple-element.4) | data formatting | bytes 2097152
  58.0 1.6 %copy.12 = f32[1,128,256]{2,1,0:T(8,128)} copy(f32[1,128,256]{2,1,0:T(8,128)} %get-tuple-element.5) | data formatting | bytes 262144

commit v2 on v1

--- a/solution.py
+++ b/solution.py
@@ -61,6 +61,13 @@
 
     load_coef.wait()
 
+    half = snps // 2
+    even = 1 - 2 * lax.rem(g, 2)
+    near, far, across = g + even, g + 2 * even, g - even
+
+    def in_range(p):
+        return jnp.logical_and(p >= 0, p < genomes)
+
     def own_block(u, carry):
         cols = pl.ds(pl.multiple_of(u * tile, tile), tile)
         block = coef[:, cols].astype(BF16)
@@ -70,26 +77,28 @@
         ext[reach, cols, :] = flat.astype(BF16)
         return carry
 
-    lax.fori_loop(0, tiles, own_block, 0)
-    pl.semaphore_wait(barrier, len(stat_peers) + ancs - 1)
-
-    distances = [d for far in range(1, reach + 1) for d in (far, -far)]
-
-    def halo_copy(d):
-        slot = reach - d
+    def halo_copy(src_slot, dst_slot, h, peer, send):
+        rows = pl.ds(h * half, half)
         return pltpu.make_async_remote_copy(
-            src_ref=ext.at[reach], dst_ref=ext.at[slot],
-            send_sem=halo_send.at[slot], recv_sem=halo_recv.at[slot],
-            device_id={"genome": jnp.clip(g + d, 0, genomes - 1)}, device_id_type=MESH,
-        )
-
-    def in_range(p):
-        return jnp.logical_and(p >= 0, p < genomes)
-
-    for d in distances:
-        @pl.when(in_range(g + d))
-        def _(d=d):
-            halo_copy(d).start()
+            src_ref=ext.at[src_slot, rows, :], dst_ref=ext.at[dst_slot, rows, :],
+            send_sem=halo_send.at[send], recv_sem=halo_recv.at[dst_slot, h],
+            device_id={"genome": jnp.clip(peer, 0, genomes - 1)}, device_id_type=MESH,
+        )
+
+    def near_copy(h):
+        return halo_copy(reach, reach - even, h, near, h)
+
+    def far_copy(d, h):
+        return halo_copy(reach, reach - d, h, g + d, (2 if d > 0 else 4) + h)
+
+    def relay_far():
+        return halo_copy(reach + even, reach - even, 0, far, 6)
+
+    def relay_near():
+        return halo_copy(reach + 2 * even, reach + even, 1, near, 7)
+
+    def arrived(slot, h):
+        halo_copy(reach, slot, h, near, 0).wait_recv()
 
     def anc_copy(k):
         return pltpu.make_async_remote_copy(
@@ -98,32 +107,40 @@
             device_id={"anc": lax.rem(a + k, ancs)}, device_id_type=MESH,
         )
 
+    def far_each(h):
+        for d in (2, -2):
+            @pl.when(in_range(g + d))
+            def _(d=d):
+                far_copy(d, h).start()
+
+    lax.fori_loop(0, tiles // 2, own_block, 0)
+    pl.semaphore_wait(barrier, len(stat_peers) + ancs - 1)
+    near_copy(0).start()
+    lax.fori_loop(tiles // 2, tiles, own_block, 0)
+    far_each(1)
+    near_copy(1).start()
+    far_each(0)
     for k in range(1, ancs):
         anc_copy(k).start()
     for u in range(tiles):
         link_copy(u).start()
     load_dosage.start()
-    load_sums.wait()
-
-    for d in distances:
-        slot = reach - d
-        chunk = 256
-
-        @pl.when(in_range(g - d))
-        def _(d=d, slot=slot):
-            halo_copy(d).wait_recv()
-
-            def widen(i, carry):
-                at = pl.multiple_of(i * chunk, chunk)
-                extf[pl.ds(pl.multiple_of(slot * snps + at, chunk), chunk), :] = (
-                    ext[slot, pl.ds(at, chunk), :].astype(F32)
-                )
-                return carry
-
-            lax.fori_loop(0, snps // chunk, widen, 0)
-
-        @pl.when(jnp.logical_not(in_range(g - d)))
-        def _(slot=slot):
+
+    chunk = 256
+
+    def widen(slot, h):
+        def piece(i, carry):
+            at = pl.multiple_of(h * half + i * chunk, chunk)
+            extf[pl.ds(pl.multiple_of(slot * snps + at, chunk), chunk), :] = (
+                ext[slot, pl.ds(at, chunk), :].astype(F32)
+            )
+            return carry
+
+        lax.fori_loop(0, half // chunk, piece, 0)
+
+    for d in (-2, -1, 1, 2):
+        @pl.when(jnp.logical_not(in_range(g + d)))
+        def _(slot=reach + d):
             def clear(i, carry):
                 at = pl.multiple_of(slot * snps + i * chunk, chunk)
                 extf[pl.ds(at, chunk), :] = jnp.zeros((chunk, traits_here), F32)
@@ -131,8 +148,45 @@
 
             lax.fori_loop(0, snps // chunk, clear, 0)
 
-    for k in range(1, ancs):
-        anc_copy(k).wait_recv()
+    arrived(reach + even, 0)
+
+    @pl.when(in_range(far))
+    def _():
+        relay_far().start()
+        arrived(reach + 2 * even, 1)
+        relay_near().start()
+
+    widen(reach + even, 0)
+
+    @pl.when(in_range(far))
+    def _():
+        widen(reach + 2 * even, 1)
+
+    @pl.when(in_range(g - 2 * even))
+    def _():
+        arrived(reach - 2 * even, 1)
+        widen(reach - 2 * even, 1)
+
+    arrived(reach + even, 1)
+    widen(reach + even, 1)
+
+    @pl.when(in_range(far))
+    def _():
+        arrived(reach + 2 * even, 0)
+        widen(reach + 2 * even, 0)
+
+    @pl.when(in_range(g - 2 * even))
+    def _():
+        arrived(reach - 2 * even, 0)
+        widen(reach - 2 * even, 0)
+
+    @pl.when(in_range(across))
+    def _():
+        for h in range(2):
+            arrived(reach - even, h)
+            widen(reach - even, h)
+
+    load_sums.wait()
 
     def band_tile(u, carry):
         link_copy(u).wait()
@@ -147,17 +201,27 @@
             )
         band = total.T
         current = coef[:, rows]
+        proposal[:, rows] = current + band - sums[:, rows]
+        return carry
+
+    lax.fori_loop(0, tiles, band_tile, 0)
+    for k in range(1, ancs):
+        anc_copy(k).wait_recv()
+
+    def propose(u, carry):
+        cols = pl.ds(pl.multiple_of(u * tile, tile), tile)
+        current = coef[:, cols]
         mean = current
         for k in range(1, ancs):
-            mean = mean + peers[k - 1, :, rows].astype(F32)
+            mean = mean + peers[k - 1, :, cols].astype(F32)
         mean = mean / ancs
-        gradient = current + band - sums[:, rows] + merging * (current - mean)
+        gradient = proposal[:, cols] + merging * (current - mean)
         value = current - step_size * gradient
-        proposal[:, rows] = value
-        row[:, rows] = jnp.sum(value * value, axis=0, keepdims=True)
-        return carry
-
-    lax.fori_loop(0, tiles, band_tile, 0)
+        proposal[:, cols] = value
+        row[:, cols] = jnp.sum(value * value, axis=0, keepdims=True)
+        return carry
+
+    lax.fori_loop(0, tiles, propose, 0)
 
     group_of = lax.broadcasted_iota(jnp.int32, (groups, snps), 0)
     mine = group_of == ids_ref[...]
@@ -231,10 +295,18 @@
     score_ref[0] = lax.fori_loop(1, genomes, add_part, partial(0)).T
 
     store.wait()
-    for d in distances:
-        @pl.when(in_range(g + d))
-        def _(d=d):
-            halo_copy(d).wait_send()
+    for h in range(2):
+        near_copy(h).wait_send()
+        for d in (2, -2):
+            @pl.when(in_range(g + d))
+            def _(d=d, h=h):
+                far_copy(d, h).wait_send()
+
+    @pl.when(in_range(far))
+    def _():
+        relay_far().wait_send()
+        relay_near().wait_send()
+
     for k in range(1, ancs):
         anc_copy(k).wait_send()
     for i in range(len(stat_peers)):
@@ -257,6 +329,7 @@
     persons_per = persons // genomes
     groups = group_weight.shape[1]
     reach = -(-width // snps)
+    assert reach == 2 and genomes % 2 == 0 and coefficients.shape[0] == 1
     tile = snps // band_start.shape[1]
     slots = 2 * reach + 1
     stat_n = genomes * traits_n - 1
@@ -291,7 +364,7 @@
             pltpu.VMEM((genomes - 1, persons_per, traits_here), BF16),
             pltpu.VMEM((genomes - 1, persons_per, traits_here), BF16),
             dma((3,)), dma((snps // tile,)), dma,
-            dma((slots,)), dma((slots,)), dma((ancs - 1,)), dma((ancs - 1,)),
+            dma((8,)), dma((slots, 2)), dma((ancs - 1,)), dma((ancs - 1,)),
             dma((stat_n,)), dma((stat_n,)), dma((genomes - 1,)), dma((genomes - 1,)),
         ],
         compiler_params=pltpu.CompilerParams(

time: 60.6 us -> 54.5 us (0.90)
  Pallas kernels: 55 us -> 49 us
    pallas_call x1, Pallas kernels: 55 us -> 49 us  [per_device(): pl.pallas_call(functools.partial(step_kernel, sizes), out_shape=(jax.Shap...]
where the time goes in v2:
time: 54.5 us; the launch traced here: 53.6 us
  Pallas kernels  49 us (90%)
  local copies, waits for them, and re-layouts  3.86 us (7%)
  between operations  0.64 us (1%)
    pallas_call x1, Pallas kernels, per_device(): pl.pallas_call(functools.partial(step_kernel, sizes), out_shape=(jax.Shap...  49 us
    unnamed x2, local copies, waits for them, and re-layouts  3.86 us

profile of v2, /device:TPU:0, one launch (start us, length us, event | category | flops | bytes accessed | tf_op | source)
XLA Modules:
  0.0 53.6 jit_solution(639743522483185223)
XLA Ops:
  0.6 49.0 %shard_map.86 = (f32[1,128,2048]{2,1,0:T(8,128)}, f32[1,128,256]{2,1,0:T(8,128)}) custom-call(f32[1,128,2048]{2,1,0:T(8,128)} %coef_hbm.1, f32[1,128,2048]{2,1,0:T(8,128)} %sums_hbm.1, bf16[1,2048,4096]{2,1,0:T(8,128)(2,1)} %link_hbm.1, s32[1,8]{1,0:T(1,128)} %starts_ref.1, s32[1,2048]{1,0:T(1,128)} %ids_ref.1, f32[1,16]{1,0:T(1,128)} %weight_ref.1, ...), custom_call_target="tpu_custom_call" | custom-call | tf_op jit(solution)/shard_map/pallas_call | solution.py:341
  49.7 2.3 %copy.11 = f32[1,128,2048]{2,1,0:T(8,128)} copy(f32[1,128,2048]{2,1,0:T(8,128)} %get-tuple-element.4) | data formatting | bytes 2097152
  52.0 1.6 %copy.12 = f32[1,128,256]{2,1,0:T(8,128)} copy(f32[1,128,256]{2,1,0:T(8,128)} %get-tuple-element.5) | data formatting | bytes 262144

commit v3 on v2

--- a/solution.py
+++ b/solution.py
@@ -19,12 +19,12 @@
 
 def step_kernel(
     sizes,
-    coef_hbm, sums_hbm, link_hbm, starts_ref, ids_ref, weight_ref, dosage_hbm,
+    coef_hbm, sums_hbm, link_hbm, starts_hbm, ids_hbm, weight_hbm, dosage_hbm,
     updated_hbm, score_ref,
-    coef, sums, link, dosage, low, ext, extf, peers, proposal, updated, updated_t, row,
-    stats_out, stats_in, part_out, part_in,
+    coef, sums, link, starts_ref, ids_ref, weight_ref, dosage, low, ext, extf, peers, proposal, updated, updated_t, row,
+    stats_out, stats_in, side_out, side_in, part_out, part_in,
     load_sem, link_sem, store_sem,
-    halo_send, halo_recv, anc_send, anc_recv, stats_send, stats_recv, part_send, part_recv,
+    halo_send, halo_recv, anc_send, anc_recv, stats_send, stats_recv, side_send, side_recv, part_send, part_recv,
 ):
     genomes, ancs, traits_n, reach, tile, groups = sizes
     traits_here, snps = coef.shape
@@ -53,6 +53,13 @@
         )
     load_sums = pltpu.make_async_copy(sums_hbm.at[0], sums, load_sem.at[1])
     load_sums.start()
+    load_small = [
+        pltpu.make_async_copy(starts_hbm, starts_ref, load_sem.at[3]),
+        pltpu.make_async_copy(ids_hbm, ids_ref, load_sem.at[4]),
+        pltpu.make_async_copy(weight_hbm, weight_ref, load_sem.at[5]),
+    ]
+    for load in load_small:
+        load.start()
     load_dosage = pltpu.make_async_copy(dosage_hbm.at[0], dosage, load_sem.at[2])
 
     def link_copy(u):
@@ -187,6 +194,8 @@
             widen(reach - even, h)
 
     load_sums.wait()
+    for load in load_small:
+        load.wait()
 
     def band_tile(u, carry):
         link_copy(u).wait()
@@ -270,29 +279,54 @@
 
     scale = 1.0 / math.sqrt(snps * genomes)
 
-    def partial(k):
-        at = pl.ds(pl.multiple_of(genome_peer(k) * persons_per, persons_per), persons_per)
+    pairs = genomes // 2
+    own_side, other_side = lax.rem(g, 2), lax.rem(near, 2)
+
+    def pair_at(i):
+        k = pairs // 2 + (1 - 2 * lax.rem(i, 2)) * ((i + 1) // 2)
+        return lax.rem(g // 2 + k + pairs, pairs)
+
+    def partial(person):
+        at = pl.ds(pl.multiple_of(person * persons_per, persons_per), persons_per)
         return jnp.dot(dosage[at, :], updated_t[...], preferred_element_type=F32) * scale
 
-    def part_copy(k):
+    def side_copy(i):
         return pltpu.make_async_remote_copy(
-            src_ref=part_out.at[k - 1], dst_ref=part_in.at[k - 1],
-            send_sem=part_send.at[k - 1], recv_sem=part_recv.at[k - 1],
-            device_id={"genome": genome_peer(k)}, device_id_type=MESH,
-        )
-
-    def send_part(k, carry):
-        part_out[k - 1] = partial(k).astype(BF16)
-        part_copy(k).start()
-        return carry
-
-    lax.fori_loop(1, genomes, send_part, 0)
-
-    def add_part(k, total):
-        part_copy(k).wait_recv()
-        return total + part_in[k - 1].astype(F32)
-
-    score_ref[0] = lax.fori_loop(1, genomes, add_part, partial(0)).T
+            src_ref=side_out.at[i], dst_ref=side_in.at[i],
+            send_sem=side_send.at[i], recv_sem=side_recv.at[i],
+            device_id={"genome": near}, device_id_type=MESH,
+        )
+
+    def part_copy(i):
+        return pltpu.make_async_remote_copy(
+            src_ref=part_out.at[i], dst_ref=part_in.at[i],
+            send_sem=part_send.at[i], recv_sem=part_recv.at[i],
+            device_id={"genome": 2 * pair_at(i) + own_side}, device_id_type=MESH,
+        )
+
+    def send_side(i, carry):
+        side_out[i] = partial(2 * pair_at(i) + other_side).astype(BF16)
+        side_copy(i).start()
+        return carry
+
+    def pair_sum(i):
+        mine_here = partial(2 * pair_at(i) + own_side)
+        side_copy(i).wait_recv()
+        return mine_here + side_in[i].astype(F32)
+
+    def send_part(i, carry):
+        part_out[i] = pair_sum(i).astype(BF16)
+        part_copy(i).start()
+        return carry
+
+    lax.fori_loop(0, pairs, send_side, 0)
+    lax.fori_loop(0, pairs - 1, send_part, 0)
+
+    def add_part(i, total):
+        part_copy(i).wait_recv()
+        return total + part_in[i].astype(F32)
+
+    score_ref[0] = lax.fori_loop(0, pairs - 1, add_part, pair_sum(pairs - 1)).T
 
     store.wait()
     for h in range(2):
@@ -312,11 +346,16 @@
     for i in range(len(stat_peers)):
         stats_copy(i).wait_send()
 
-    def sent_part(k, carry):
-        part_copy(k).wait_send()
-        return carry
-
-    lax.fori_loop(1, genomes, sent_part, 0)
+    def sent_side(i, carry):
+        side_copy(i).wait_send()
+        return carry
+
+    def sent_part(i, carry):
+        part_copy(i).wait_send()
+        return carry
+
+    lax.fori_loop(0, pairs, sent_side, 0)
+    lax.fori_loop(0, pairs - 1, sent_part, 0)
 
 
 def per_device(coefficients, sumstats, linkage, band_start, group_ids, group_weight, dosage):
@@ -332,11 +371,12 @@
     assert reach == 2 and genomes % 2 == 0 and coefficients.shape[0] == 1
     tile = snps // band_start.shape[1]
     slots = 2 * reach + 1
+    pairs = genomes // 2
     stat_n = genomes * traits_n - 1
     sizes = (genomes, ancs, traits_n, reach, tile, groups)
     anyspace = pl.BlockSpec(memory_space=pl.ANY)
+    hbm = pl.BlockSpec(memory_space=pltpu.HBM)
     vmem = pl.BlockSpec(memory_space=pltpu.VMEM)
-    smem = pl.BlockSpec(memory_space=pltpu.SMEM)
     dma = pltpu.SemaphoreType.DMA
     return pl.pallas_call(
         functools.partial(step_kernel, sizes),
@@ -344,12 +384,15 @@
             jax.ShapeDtypeStruct((1, traits_here, snps), F32),
             jax.ShapeDtypeStruct((1, traits_here, persons_per), F32),
         ),
-        in_specs=[anyspace, anyspace, anyspace, smem, vmem, vmem, anyspace],
+        in_specs=[hbm] * 7,
         out_specs=(anyspace, vmem),
         scratch_shapes=[
             pltpu.VMEM((traits_here, snps), F32),
             pltpu.VMEM((traits_here, snps), F32),
             pltpu.VMEM((snps, width), BF16),
+            pltpu.SMEM(band_start.shape, jnp.int32),
+            pltpu.VMEM(group_ids.shape, jnp.int32),
+            pltpu.VMEM(group_weight.shape, F32),
             pltpu.VMEM((persons, snps), BF16),
             pltpu.VMEM((traits_here, snps), BF16),
             pltpu.VMEM((slots, snps, traits_here), BF16),
@@ -361,14 +404,16 @@
             pltpu.VMEM((1, snps), F32),
             pltpu.VMEM((groups, 128), F32),
             pltpu.VMEM((stat_n, groups, 128), F32),
-            pltpu.VMEM((genomes - 1, persons_per, traits_here), BF16),
-            pltpu.VMEM((genomes - 1, persons_per, traits_here), BF16),
-            dma((3,)), dma((snps // tile,)), dma,
+            pltpu.VMEM((pairs, persons_per, traits_here), BF16),
+            pltpu.VMEM((pairs, persons_per, traits_here), BF16),
+            pltpu.VMEM((pairs - 1, persons_per, traits_here), BF16),
+            pltpu.VMEM((pairs - 1, persons_per, traits_here), BF16),
+            dma((6,)), dma((snps // tile,)), dma,
             dma((8,)), dma((slots, 2)), dma((ancs - 1,)), dma((ancs - 1,)),
-            dma((stat_n,)), dma((stat_n,)), dma((genomes - 1,)), dma((genomes - 1,)),
+            dma((stat_n,)), dma((stat_n,)), dma((pairs,)), dma((pairs,)), dma((pairs - 1,)), dma((pairs - 1,)),
         ],
         compiler_params=pltpu.CompilerParams(
-            collective_id=0, has_side_effects=True, vmem_limit_bytes=56 * 1024 * 1024
+            collective_id=0, has_side_effects=True, vmem_limit_bytes=52 * 1024 * 1024
         ),
     )(coefficients, sumstats, linkage, band_start, group_ids, group_weight, dosage)
 

time: 54.5 us -> 52.2 us (0.958); the launches traced: 53.6 us -> 51.9 us
  Pallas kernels: 49 us -> 47.7 us
    pallas_call x1, Pallas kernels: 49 us -> 47.7 us  [per_device(): pl.pallas_call(functools.partial(step_kernel, sizes), out_shape=(jax.Shap...]
    unnamed x2 -> x8, local copies, waits for them, and re-layouts: 3.86 us -> 3.63 us
where the time goes in v3:
time: 52.2 us; the launch traced here: 51.9 us
  Pallas kernels  47.7 us (91%)
  local copies, waits for them, and re-layouts  3.63 us (7%)
  between operations  0.65 us (1%)
    pallas_call x1, Pallas kernels, per_device(): pl.pallas_call(functools.partial(step_kernel, sizes), out_shape=(jax.Shap...  47.7 us
    unnamed x8, local copies, waits for them, and re-layouts  3.63 us

profile of v3, /device:TPU:0, one launch (start us, length us, event | category | flops | bytes accessed | tf_op | source)
XLA Modules:
  0.0 51.9 jit_solution(7095447619840568328)
XLA Ops:
  0.6 0.0 copy-start
  0.6 0.7 %copy-done = s32[1,2048]{1,0:T(1,128)S(1)} copy-done((s32[1,2048]{1,0:T(1,128)S(1)}, s32[1,2048]{1,0:T(1,128)}, u32[]{:S(2)}) %copy-start) | copy-done | bytes 8216
  1.3 0.0 copy-start.1
  1.3 0.7 %copy-done.1 = s32[1,8]{1,0:T(1,128)S(1)} copy-done((s32[1,8]{1,0:T(1,128)S(1)}, s32[1,8]{1,0:T(1,128)}, u32[]{:S(2)}) %copy-start.1) | copy-done | bytes 56
  2.0 0.0 copy-start.2
  2.0 0.7 %copy-done.2 = f32[1,16]{1,0:T(1,128)S(1)} copy-done((f32[1,16]{1,0:T(1,128)S(1)}, f32[1,16]{1,0:T(1,128)}, u32[]{:S(2)}) %copy-start.2) | copy-done | bytes 88
  2.6 47.7 %shard_map.86 = (f32[1,128,2048]{2,1,0:T(8,128)S(1)}, f32[1,128,256]{2,1,0:T(8,128)S(1)}) custom-call(f32[1,128,2048]{2,1,0:T(8,128)} %coef_hbm.1, f32[1,128,2048]{2,1,0:T(8,128)} %sums_hbm.1, bf16[1,2048,4096]{2,1,0:T(8,128)(2,1)} %link_hbm.1, s32[1,8]{1,0:T(1,128)S(1)} %copy-done.1, s32[1,2048]{1,0:T(1,128)S(1)} %copy-done, f32[1,16]{1,0:T(1,128)S(1)} %copy-done.2, ...), custom_call_target="tpu_custom_call" | custom-call | tf_op jit(solution)/shard_map/pallas_call | solution.py:381
  50.3 1.0 %copy.11 = f32[1,128,2048]{2,1,0:T(8,128)} copy(f32[1,128,2048]{2,1,0:T(8,128)S(1)} %get-tuple-element.4) | data formatting | bytes 2097152
  51.3 0.7 %copy.12 = f32[1,128,256]{2,1,0:T(8,128)} copy(f32[1,128,256]{2,1,0:T(8,128)S(1)} %get-tuple-element.5) | data formatting | bytes 262144
Async XLA Ops:
  0.6 0.7 %copy-start = (s32[1,2048]{1,0:T(1,128)S(1)}, s32[1,2048]{1,0:T(1,128)}, u32[]{:S(2)}) copy-start(s32[1,2048]{1,0:T(1,128)} %ids_hbm.1) | copy-start | bytes 24580
  1.3 0.7 %copy-start.1 = (s32[1,8]{1,0:T(1,128)S(1)}, s32[1,8]{1,0:T(1,128)}, u32[]{:S(2)}) copy-start(s32[1,8]{1,0:T(1,128)} %starts_hbm.1) | copy-start | bytes 100
  2.0 0.7 %copy-start.2 = (f32[1,16]{1,0:T(1,128)S(1)}, f32[1,16]{1,0:T(1,128)}, u32[]{:S(2)}) copy-start(f32[1,16]{1,0:T(1,128)} %weight_hbm.1) | copy-start | bytes 196

commit v4 on v3

--- a/solution.py
+++ b/solution.py
@@ -120,10 +120,10 @@
             def _(d=d):
                 far_copy(d, h).start()
 
-    lax.fori_loop(0, tiles // 2, own_block, 0)
+    lax.fori_loop(0, tiles // 2, own_block, 0, unroll=2)
     pl.semaphore_wait(barrier, len(stat_peers) + ancs - 1)
     near_copy(0).start()
-    lax.fori_loop(tiles // 2, tiles, own_block, 0)
+    lax.fori_loop(tiles // 2, tiles, own_block, 0, unroll=2)
     far_each(1)
     near_copy(1).start()
     far_each(0)
@@ -143,7 +143,7 @@
             )
             return carry
 
-        lax.fori_loop(0, half // chunk, piece, 0)
+        lax.fori_loop(0, half // chunk, piece, 0, unroll=2)
 
     for d in (-2, -1, 1, 2):
         @pl.when(jnp.logical_not(in_range(g + d)))
@@ -213,7 +213,7 @@
         proposal[:, rows] = current + band - sums[:, rows]
         return carry
 
-    lax.fori_loop(0, tiles, band_tile, 0)
+    lax.fori_loop(0, tiles, band_tile, 0, unroll=2)
     for k in range(1, ancs):
         anc_copy(k).wait_recv()
 
@@ -230,7 +230,7 @@
         row[:, cols] = jnp.sum(value * value, axis=0, keepdims=True)
         return carry
 
-    lax.fori_loop(0, tiles, propose, 0)
+    lax.fori_loop(0, tiles, propose, 0, unroll=2)
 
     group_of = lax.broadcasted_iota(jnp.int32, (groups, snps), 0)
     mine = group_of == ids_ref[...]
@@ -273,7 +273,7 @@
         updated_t[cols, :] = value.T.astype(BF16)
         return carry
 
-    lax.fori_loop(0, tiles, shrink_tile, 0)
+    lax.fori_loop(0, tiles, shrink_tile, 0, unroll=2)
     store = pltpu.make_async_copy(updated, updated_hbm.at[0], store_sem)
     store.start()
 

time: 52.2 us -> 51.6 us (0.989)
  Pallas kernels: 47.7 us -> 47.1 us
    pallas_call x1, Pallas kernels: 47.7 us -> 47.1 us  [per_device(): pl.pallas_call(functools.partial(step_kernel, sizes), out_shape=(jax.Shap...]
where the time goes in v4:
time: 51.6 us; the launch traced here: 51.4 us
  Pallas kernels  47.1 us (91%)
  local copies, waits for them, and re-layouts  3.63 us (7%)
  between operations  0.65 us (1%)
    pallas_call x1, Pallas kernels, per_device(): pl.pallas_call(functools.partial(step_kernel, sizes), out_shape=(jax.Shap...  47.1 us
    unnamed x8, local copies, waits for them, and re-layouts  3.63 us

profile of v4, /device:TPU:0, one launch (start us, length us, event | category | flops | bytes accessed | tf_op | source)
XLA Modules:
  0.0 51.4 jit_solution(15492033870777654878)
XLA Ops:
  0.6 0.0 copy-start
  0.6 0.7 %copy-done = s32[1,2048]{1,0:T(1,128)S(1)} copy-done((s32[1,2048]{1,0:T(1,128)S(1)}, s32[1,2048]{1,0:T(1,128)}, u32[]{:S(2)}) %copy-start) | copy-done | bytes 8216
  1.3 0.0 copy-start.1
  1.3 0.7 %copy-done.1 = s32[1,8]{1,0:T(1,128)S(1)} copy-done((s32[1,8]{1,0:T(1,128)S(1)}, s32[1,8]{1,0:T(1,128)}, u32[]{:S(2)}) %copy-start.1) | copy-done | bytes 56
  2.0 0.0 copy-start.2
  2.0 0.7 %copy-done.2 = f32[1,16]{1,0:T(1,128)S(1)} copy-done((f32[1,16]{1,0:T(1,128)S(1)}, f32[1,16]{1,0:T(1,128)}, u32[]{:S(2)}) %copy-start.2) | copy-done | bytes 88
  2.6 47.1 %shard_map.86 = (f32[1,128,2048]{2,1,0:T(8,128)S(1)}, f32[1,128,256]{2,1,0:T(8,128)S(1)}) custom-call(f32[1,128,2048]{2,1,0:T(8,128)} %coef_hbm.1, f32[1,128,2048]{2,1,0:T(8,128)} %sums_hbm.1, bf16[1,2048,4096]{2,1,0:T(8,128)(2,1)} %link_hbm.1, s32[1,8]{1,0:T(1,128)S(1)} %copy-done.1, s32[1,2048]{1,0:T(1,128)S(1)} %copy-done, f32[1,16]{1,0:T(1,128)S(1)} %copy-done.2, ...), custom_call_target="tpu_custom_call" | custom-call | tf_op jit(solution)/shard_map/pallas_call | solution.py:381
  49.7 1.0 %copy.11 = f32[1,128,2048]{2,1,0:T(8,128)} copy(f32[1,128,2048]{2,1,0:T(8,128)S(1)} %get-tuple-element.4) | data formatting | bytes 2097152
  50.7 0.7 %copy.12 = f32[1,128,256]{2,1,0:T(8,128)} copy(f32[1,128,256]{2,1,0:T(8,128)S(1)} %get-tuple-element.5) | data formatting | bytes 262144
Async XLA Ops:
  0.6 0.7 %copy-start = (s32[1,2048]{1,0:T(1,128)S(1)}, s32[1,2048]{1,0:T(1,128)}, u32[]{:S(2)}) copy-start(s32[1,2048]{1,0:T(1,128)} %ids_hbm.1) | copy-start | bytes 24580
  1.3 0.7 %copy-start.1 = (s32[1,8]{1,0:T(1,128)S(1)}, s32[1,8]{1,0:T(1,128)}, u32[]{:S(2)}) copy-start(s32[1,8]{1,0:T(1,128)} %starts_hbm.1) | copy-start | bytes 100
  2.0 0.7 %copy-start.2 = (f32[1,16]{1,0:T(1,128)S(1)}, f32[1,16]{1,0:T(1,128)}, u32[]{:S(2)}) copy-start(f32[1,16]{1,0:T(1,128)} %weight_hbm.1) | copy-start | bytes 196
